TPU v7x, 128 devices: a whole 4x4x4 slice. The times are simulated.
128 devices in a mesh: row: 16 (over x, y_lo, core), col: 8 (over y_hi, z).
Axes of the slice: x: 4, y: 4 (y_hi: 2, y_lo: 2; y = y_hi * 2 + y_lo), z: 4, core: 2. Of those that a mesh axis runs over, the one named last changes fastest.
Arguments:
- vectors: bfloat16 [64, 1024, 512], P('col', 'row'), may hold values from -6 to 6
- right_factors: bfloat16 [64, 64, 1024, 128], P('row', 'col'), may hold values from -0.1875 to 0.1875
- left_factors: bfloat16 [64, 64, 1024, 128], P('row', 'col'), may hold values from -0.09375 to 0.09375
- tile_ranks: int32 [64, 64], P('row', 'col'), may hold values from 16 to 128
- owner_map: int32 [64], replicated, may hold values from 0 to 63, as said below
Outputs:
- applied: bfloat16 [64, 1024, 512], P('row', 'col')
Inputs may be any that keep to these rules, and one draw needn't show every extreme that they name: owner_map is a permutation of 0 to 63; the 4 stored tile rows held by index i of row (stored rows i * 4 to i * 4 + 3) belong to 4 different indices of row of applied, i + c mod 16 for the same 4 offsets c at every i.
All inputs are finite; a program needn't handle non-finite values.
Results may differ from a plain program's by a relative error of at most 0.0066.
Values may be sent and summed in bfloat16 or wider, within the bound.
A program may use at most 128 MiB of HBM per device.

v0:
```python
import jax
import jax.numpy as jnp
from jax import lax
from jax.sharding import PartitionSpec as P


def split_up(x, dim, peers):
    before, after = (x.shape[:dim], x.shape[dim + 1 :])
    return jnp.moveaxis(x.reshape(*before, peers, -1, *after), dim, 0)


def sent_and_summed(x, axis, dim):
    pieces = split_up(x, dim, lax.axis_size(axis))
    arrived = lax.all_to_all(pieces, axis, split_axis=0, concat_axis=0, tiled=True)
    return arrived.astype(jnp.float32).sum(axis=0)


def masked_coeffs(products, tile_ranks, rank_width):
    columns = jnp.arange(rank_width, dtype=jnp.int32)
    kept_mask = columns[None, None, :] < tile_ranks[:, :, None]
    return jnp.where(kept_mask[:, :, :, None], products, 0.0).astype(jnp.bfloat16)


def build_buffer(payload, owner_map, cycle_size):
    held_rows = payload.shape[0]
    own_rows = lax.dynamic_slice_in_dim(owner_map, lax.axis_index("row") * held_rows, held_rows)
    target = own_rows // held_rows
    devices = jnp.arange(cycle_size, dtype=jnp.int32)
    matches = target[None, :] == devices[:, None]
    present = jnp.any(matches, axis=1)
    source_slot = jnp.sum(
        jnp.where(matches, jnp.arange(held_rows, dtype=jnp.int32)[None, :], 0), axis=1
    )
    picked = jnp.take(payload, source_slot, axis=0)
    return jnp.where(present[:, None, None], picked, jnp.zeros_like(picked))


def pick_rows(received, owner_map, held_rows):
    wanted = lax.axis_index("row") * held_rows + jnp.arange(held_rows, dtype=jnp.int32)
    matches = owner_map[None, :] == wanted[:, None]
    anchor = jnp.sum(
        jnp.where(matches, jnp.arange(owner_map.shape[0], dtype=jnp.int32)[None, :], 0), axis=1
    )
    return jnp.take(received, anchor // held_rows, axis=0)


def on_device(vectors, right_factors, left_factors, tile_ranks, owner_map):
    held_rows = right_factors.shape[0]
    rank_width = right_factors.shape[3]
    cycle_size = lax.axis_size("row")
    products = jnp.einsum(
        "ikbr,kbv->ikrv",
        right_factors,
        lax.all_gather(vectors, "row", axis=1, tiled=True),
        preferred_element_type=jnp.float32,
    )
    coeffs = masked_coeffs(products, tile_ranks, rank_width)
    partial_rows = jnp.einsum(
        "ikbr,ikrv->ibv", left_factors, coeffs, preferred_element_type=jnp.float32
    )
    summed = sent_and_summed(partial_rows.astype(jnp.bfloat16), "col", 1).astype(jnp.bfloat16)
    buffer = build_buffer(summed, owner_map, cycle_size)
    received = lax.all_to_all(buffer, "row", split_axis=0, concat_axis=0, tiled=True)
    applied = pick_rows(received, owner_map, held_rows)
    return applied


def solution(mesh):
    placed = (
        P("col", "row", None),
        P("row", "col", None, None),
        P("row", "col", None, None),
        P("row", "col"),
        P(),
    )
    return jax.shard_map(
        on_device, mesh=mesh, in_specs=placed, out_specs=P("row", "col", None), check_vma=False
    )
```

profile of v0, /device:TPU:1, one launch (start us, length us, event | category | flops | bytes accessed | tf_op | source)
XLA Modules:
  0.0 187.5 jit_solution(1948998117102520125)
XLA Ops:
  6.5 0.0 all-gather.2.cloned.1.call-start
  6.5 0.7 all-gather.2.cloned.1.call-update
  7.3 0.8 iota_compare_fusion
  8.0 56.6 %all-gather.2.cloned.1.call-done = bf16[8,1024,512]{2,1,0:T(8,128)(2,1)} async-done(((bf16[8,64,512]{2,1,0:T(8,128)(2,1)}), bf16[8,1024,512]{2,1,0:T(8,128)(2,1)}) %all-gather.2.cloned.1.call-update) | async-done | bytes 8388624 | tf_op jit(solution)/shard_map/all_gather | solution.py:54
  64.7 16.4 %fusion.5 = bf16[4,64,8,8,128]{4,3,2,1,0:T(8,128)(2,1)} fusion(bf16[4,8,1024,128]{3,2,1,0:T(8,128)(2,1)} %param.7, pred[4,8,128]{2,1,0:T(8,128)(4,1)S(1)} %iota_compare_fusion, bf16[4,8,1024,128]{3,2,1,0:T(8,128)(2,1)} %param.6, bf16[8,1024,512]{2,1,0:T(8,128)(2,1)} %all-gather.2.cloned.1.call-done), kind=kOutput, calls=%fused_computation.8 | convolution fusion | flops 8596226048 | bytes 29364224 | tf_op jit(solution)/shard_map/ikbr,ikrv->ibv/dot_general | solution.py:58
  81.0 5.3 %copy.18 = bf16[4,64,8,8,128]{4,3,1,0,2:T(8,128)(2,1)} copy(bf16[4,64,8,8,128]{4,3,2,1,0:T(8,128)(2,1)} %fusion.5) | data formatting | bytes 8388608 | tf_op jit(solution)/shard_map/reshape | solution.py:9
  86.3 0.0 copy-start
  86.3 6.6 %all-to-all-start = ((bf16[8,4,128,512]{2,3,1,0:T(8,128)(2,1)}), bf16[8,4,128,512]{2,3,1,0:T(8,128)(2,1)}, u32[]{:S(2)}, u32[]{:S(2)}) async-start(bf16[8,4,128,512]{2,3,1,0:T(8,128)(2,1)} %bitcast.48), calls=%async_computation | async-start | bytes 8388608 | tf_op jit(solution)/shard_map/all_to_all | solution.py:14
  92.9 0.0 copy-done
  92.9 0.1 and_select_fusion.1
  93.0 0.1 select_reduce_fusion
  93.1 0.1 fusion.16
  93.2 48.5 %all-to-all-done = bf16[8,4,128,512]{2,3,1,0:T(8,128)(2,1)} async-done(((bf16[8,4,128,512]{2,3,1,0:T(8,128)(2,1)}), bf16[8,4,128,512]{2,3,1,0:T(8,128)(2,1)}, u32[]{:S(2)}, u32[]{:S(2)}) %all-to-all-start) | async-done | bytes 4194336 | tf_op jit(solution)/shard_map/all_to_all | solution.py:14
  141.7 2.9 %reduce_sum.36 = bf16[4,128,512]{1,2,0:T(8,128)(2,1)S(1)} reduce(bf16[8,4,128,512]{2,3,1,0:T(8,128)(2,1)} %all-to-all-done, bf16[]{:T(256)} %constant.65.clone.1), dimensions={0}, to_apply=%region_3.4 | reduce | flops 1835008 | bytes 4718594 | tf_op jit(solution)/shard_map/reduce_sum | solution.py:15
  144.6 0.2 copy.13
  144.8 0.7 gather_fusion
  145.5 1.7 select_select_fusion
  147.1 5.2 %all-to-all-start.1 = ((bf16[16,128,512]{2,1,0:T(8,128)(2,1)}), bf16[16,128,512]{2,1,0:T(8,128)(2,1)S(1)}, u32[]{:S(2)}, u32[]{:S(2)}) async-start(bf16[16,128,512]{2,1,0:T(8,128)(2,1)} %select_select_fusion), calls=%async_computation.1 | async-start | bytes 4194304 | tf_op jit(solution)/shard_map/all_to_all | solution.py:63
  152.4 0.2 select_reduce_fusion.1
  152.6 26.6 %all-to-all-done.1 = bf16[16,128,512]{2,1,0:T(8,128)(2,1)S(1)} async-done(((bf16[16,128,512]{2,1,0:T(8,128)(2,1)}), bf16[16,128,512]{2,1,0:T(8,128)(2,1)S(1)}, u32[]{:S(2)}, u32[]{:S(2)}) %all-to-all-start.1) | async-done | bytes 2097184 | tf_op jit(solution)/shard_map/all_to_all | solution.py:63
  179.2 0.6 gather_fusion.1
  179.8 0.9 broadcast_select_fusion
  (7 shorter events, 0.1 us)
Async XLA Ops:
  6.5 58.1 %all-gather.2.cloned.1.call-start = ((), (), s32[]{:S(2)}) async-start(), calls=%async_computation.2 | async-start | bytes 8912896 | tf_op jit(solution)/shard_map/all_gather | solution.py:54
  86.3 6.6 %copy-start = (s32[64]{0:T(128)S(1)}, s32[64]{0:T(128)}, u32[]{:S(2)}) copy-start(s32[64]{0:T(128)} %param.9) | copy-start | bytes 772
  86.3 55.4 %all-to-all-start = ((bf16[8,4,128,512]{2,3,1,0:T(8,128)(2,1)}), bf16[8,4,128,512]{2,3,1,0:T(8,128)(2,1)}, u32[]{:S(2)}, u32[]{:S(2)}) async-start(bf16[8,4,128,512]{2,3,1,0:T(8,128)(2,1)} %bitcast.48), calls=%async_computation | async-start | bytes 8388608 | tf_op jit(solution)/shard_map/all_to_all | solution.py:14
  147.1 32.1 %all-to-all-start.1 = ((bf16[16,128,512]{2,1,0:T(8,128)(2,1)}), bf16[16,128,512]{2,1,0:T(8,128)(2,1)S(1)}, u32[]{:S(2)}, u32[]{:S(2)}) async-start(bf16[16,128,512]{2,1,0:T(8,128)(2,1)} %select_select_fusion), calls=%async_computation.1 | async-start | bytes 4194304 | tf_op jit(solution)/shard_map/all_to_all | solution.py:63
Sparse Core Ops, SparseCore 0:
  9.0 55.6 all-gather.1
where the time goes:
time: 189 us; the launch traced here: 188 us
  waiting for transfers between devices  132 us (70%)
  matrix products  16.4 us (9%)
  between operations  13.4 us (7%)
  starting transfers between devices  11.9 us (6%)
  local copies, waits for them, and re-layouts  6.76 us (4%)
  other arithmetic  6.68 us (4%)
    all_gather x1, waiting for transfers between devices, on_device(): lax.all_gather(vectors, 'row', axis=1, tiled=True)  56.6 us
    all_to_all x1, waiting for transfers between devices, sent_and_summed(): lax.all_to_all(pieces, axis, split_axis=0, concat_axis=0, tiled=True)  48.5 us
    all_to_all x1, waiting for transfers between devices, on_device(): lax.all_to_all(buffer, 'row', split_axis=0, concat_axis=0, tiled=True)  26.6 us
    dot_general x1, matrix products, on_device(): jnp.einsum('ikbr,ikrv->ibv', left_factors, coeffs, preferred_element_type...  16.4 us
    all_to_all x1, starting transfers between devices, sent_and_summed(): lax.all_to_all(pieces, axis, split_axis=0, concat_axis=0, tiled=True)  6.62 us
    reshape x1, local copies, waits for them, and re-layouts, split_up(): return jnp.moveaxis(x.reshape(*before, peers, -1, *after), dim, 0)  5.27 us
    all_to_all x1, starting transfers between devices, on_device(): lax.all_to_all(buffer, 'row', split_axis=0, concat_axis=0, tiled=True)  5.25 us
  transfers between devices with their start and end apart: 3, of which 3 were waited for; matrix products, arithmetic and copies ran while one was open for 1% of the time, Pallas kernels for 0%

commit v1 on v0

v1 whole, which is shorter than its diff:
```python
import functools

import jax
import jax.numpy as jnp
from jax import lax
from jax.experimental import pallas as pl
from jax.experimental.pallas import tpu as pltpu
from jax.sharding import PartitionSpec as P

MESH = pl.DeviceIdType.MESH
F32, BF16, I32 = jnp.float32, jnp.bfloat16, jnp.int32

NX, STEP_X, STEP_Y, STEP_CORE = 4, 4, 2, 1
NZ, NYH = 4, 2
CHUNKS = (256, 256)


def kernel(dims, *refs):
    held, ncol, blk, rank, share = dims
    nrow = blk // share
    ndst = NZ * NYH
    sub = blk // ndst
    piece = sub // nrow
    nt = len(CHUNKS)
    starts = [sum(CHUNKS[:t]) for t in range(nt)]
    refs = list(refs)
    vec, rf, lf, ranks, omap, out = refs[:6]
    raw, rt, lt, ssem, rsem, lsem, csem = refs[6:13]
    per = [refs[13 + 13 * t : 26 + 13 * t] for t in range(nt)]
    V, C, part, s1, s2, s3, s4, zown, fin, r1, send2, r2, _ = [list(a) for a in zip(*per)]

    i, d = lax.axis_index("row"), lax.axis_index("col")
    z, yh = lax.rem(d, NZ), lax.div(d, NZ)
    x = lax.div(i, STEP_X)
    inner = lax.rem(i, STEP_X)

    def at_x(dx):
        return lax.rem(x + dx + NX, NX) * STEP_X + inner

    def flip_y(r):
        return jnp.where(lax.rem(lax.div(r, STEP_Y), 2) == 0, r + STEP_Y, r - STEP_Y)

    def flip_core(r):
        return jnp.where(lax.rem(r, 2) == 0, r + 1, r - 1)

    def at_z(dz):
        return lax.rem(z + dz + NZ, NZ)

    iy, ic = flip_y(i), flip_core(i)
    xp, xm = at_x(1), at_x(-1)
    zp, zm, zo = at_z(1), at_z(-1), at_z(2)
    yo = 1 - yh

    loads = {}

    def load(name, src, dst):
        copy = pltpu.make_async_copy(src, dst, lsem.at[len(loads)])
        copy.start()
        loads[name] = copy

    def rows_of(t, j, k0=0, k1=ncol):
        return V[t].at[pl.ds(k0, k1 - k0), pl.ds(pl.multiple_of(j * share, share), share), :]

    for t in range(nt):
        load(("v", t), vec.at[:, :, pl.ds(starts[t], CHUNKS[t])], rows_of(t, i))
    for k in range(ncol):
        load(("r", k), rf.at[:, k], raw.at[:, k])
    load("l", lf, lt)

    bar = pltpu.get_barrier_semaphore()
    for m in range(1, nrow):
        pl.semaphore_signal(bar, 1, device_id={"row": lax.rem(i + m, nrow)}, device_id_type=MESH)
    for c in (yh * NZ + zp, yh * NZ + zm, yo * NZ + z):
        pl.semaphore_signal(bar, 1, device_id={"col": c}, device_id_type=MESH)
    pl.semaphore_wait(bar, nrow - 1 + 3)

    own = [omap[held * i + s] for s in range(held)]
    off = [lax.rem(lax.div(o, held) - i + nrow, nrow) for o in own]
    place = [sum((off[s] > off[u] if u > s else off[s] >= off[u]).astype(I32) for u in range(held) if u != s) for s in range(held)]
    sig = [sum(jnp.where(place[s] == q, s, 0) for s in range(held)) for q in range(held)]
    offq = [sum(jnp.where(place[s] == q, off[s], 0) for s in range(held)) for q in range(held)]
    lands = []
    for q in range(held):
        src = lax.rem(i - offq[q] + nrow, nrow)
        there = [omap[held * src + s] for s in range(held)]
        lands.append(sum(jnp.where(lax.div(o, held) == i, lax.rem(o, held), 0) for o in there))
    qof = [lax.rem(sum(jnp.where(lands[q] == o, q, 0) for q in range(held)), held) for o in range(held)]

    sent = {}

    def send(name, src, dst, dev):
        n = len(sent)
        copy = pltpu.make_async_remote_copy(
            src_ref=src, dst_ref=dst, send_sem=ssem.at[n], recv_sem=rsem.at[n], device_id=dev, device_id_type=MESH
        )
        copy.start()
        sent[name] = copy

    def got(*name):
        sent[name].wait_recv()

    def share_to(name, t, j, row, k0=0, k1=ncol):
        send(name, rows_of(t, j, k0, k1), rows_of(t, j, k0, k1), {"row": row})

    half = ncol // 2

    def a_own(t):
        loads["v", t].wait()
        share_to(("y", t), t, i, iy)
        share_to(("xp0", t), t, i, xp)
        share_to(("xm0", t), t, i, xm)
        share_to(("d0", t), t, i, ic)

    def a_part(t):
        got("y", t)
        share_to(("xp1", t), t, iy, xp)
        share_to(("xm1", t), t, iy, xm)
        share_to(("d1", t), t, iy, ic)

    def a_pass(t, n):
        lo, hi = (xm, xp) if n == 0 else (flip_y(xm), flip_y(xp))
        got(f"xp{n}", t)
        share_to((f"fp{n}", t), t, lo, xp, 0, half)
        share_to((f"dm{n}", t), t, lo, ic)
        got(f"xm{n}", t)
        share_to((f"fm{n}", t), t, hi, xm, half, ncol)
        share_to((f"dp{n}", t), t, hi, ic)

    def a_last(t, n):
        far = at_x(2) if n == 0 else flip_y(at_x(2))
        got(f"fp{n}", t)
        share_to((f"df{n}", t), t, far, ic, 0, half)
        got(f"fm{n}", t)
        share_to((f"dg{n}", t), t, far, ic, half, ncol)

    def a_end(t):
        for n in range(2):
            for name in ("d", "dm", "dp", "df", "dg"):
                got(f"{name}{n}", t)

    def turn(k0, k1):
        for k in range(k0, k1):
            loads["r", k].wait()

        def one(n, carry):
            k, s = k0 + lax.div(n, held), lax.rem(n, held)
            rt[k, pl.ds(pl.multiple_of(s * rank, rank), rank), :] = raw[s, k].T
            return carry

        lax.fori_loop(0, (k1 - k0) * held, one, 0)

    def m1(t):
        width = CHUNKS[t]

        def one(k, carry):
            acc = jnp.dot(rt[k], V[t][k], preferred_element_type=F32)
            for s in range(held):
                kept = lax.broadcasted_iota(I32, (rank, width), 0) < ranks[s, k]
                C[t][s, pl.ds(pl.multiple_of(k * rank, rank), rank), :] = jnp.where(
                    kept, acc[s * rank : (s + 1) * rank], 0.0
                ).astype(BF16)
            return carry

        lax.fori_loop(0, ncol, one, 0)

    def m2(t, q, blocks):
        slot = sig[q]
        left = [
            jnp.concatenate(
                [lt[slot, k, pl.ds(pl.multiple_of((y * NZ + w) * sub, sub), sub), :] for k in range(ncol)], axis=1
            )
            for y, w in blocks
        ]
        res = jnp.dot(jnp.concatenate(left, axis=0), C[t][slot], preferred_element_type=F32).astype(BF16)
        for n, (y, w) in enumerate(blocks):
            part[t][q, y, w] = res[n * sub : (n + 1) * sub]

    def col_z(w):
        return {"col": yh * NZ + w}

    def b_first(t, q):
        m2(t, q, [(0, zo), (1, zo), (1, zp), (0, zm)])
        send(("s1p", t, q), part[t].at[q, 0, zo], s1[t].at[q, 0], col_z(zp))
        send(("s1m", t, q), part[t].at[q, 1, zo], s1[t].at[q, 1], col_z(zm))
        send(("s2p", t, q), part[t].at[q, 1, zp], s2[t].at[q, 0], col_z(zp))
        send(("s2m", t, q), part[t].at[q, 0, zm], s2[t].at[q, 1], col_z(zm))
        m2(t, q, [(0, zp), (1, zm), (0, z), (1, z)])

    def b_pass(t, q):
        got("s1p", t, q)
        part[t][q, 0, zp] = (part[t][q, 0, zp].astype(F32) + s1[t][q, 0].astype(F32)).astype(BF16)
        send(("s3p", t, q), part[t].at[q, 0, zp], s3[t].at[q, 0], col_z(zp))
        got("s1m", t, q)
        part[t][q, 1, zm] = (part[t][q, 1, zm].astype(F32) + s1[t][q, 1].astype(F32)).astype(BF16)
        send(("s3m", t, q), part[t].at[q, 1, zm], s3[t].at[q, 1], col_z(zm))

    def b_sum(t, q):
        got("s2p", t, q)
        got("s2m", t, q)
        got("s3p", t, q)
        got("s3m", t, q)
        low = part[t][q, 0, z].astype(F32) + (s3[t][q, 0].astype(F32) + s2[t][q, 1].astype(F32))
        high = part[t][q, 1, z].astype(F32) + (s2[t][q, 0].astype(F32) + s3[t][q, 1].astype(F32))
        here = yh == 0
        zown[t][q] = jnp.where(here, low, high)
        part[t][q, 0, z] = jnp.where(here, high, low).astype(BF16)
        send(("s4", t, q), part[t].at[q, 0, z], s4[t].at[q], {"col": yo * NZ + z})

    def b_end(t, q):
        got("s4", t, q)
        total = (zown[t][q] + s4[t][q].astype(F32)).reshape(nrow, piece, CHUNKS[t]).astype(BF16)
        fin[t][:, q] = total
        r1[t][0, q] = total[0]

    def spread(t, phase, src, dst):
        for m in range(1, nrow):
            pltpu.make_async_remote_copy(
                src_ref=src.at[m],
                dst_ref=dst.at[m],
                send_sem=csem.at[t, phase, 0],
                recv_sem=csem.at[t, phase, 1],
                device_id={"row": lax.rem(i + m, nrow)},
                device_id_type=MESH,
            ).start()

    def spread_all(t, phase, src, dst):
        return pltpu.make_async_remote_copy(
            src_ref=src.at[pl.ds(1, nrow - 1)],
            dst_ref=dst.at[pl.ds(1, nrow - 1)],
            send_sem=csem.at[t, phase, 0],
            recv_sem=csem.at[t, phase, 1],
            device_id={"row": lax.rem(i + 1, nrow)},
            device_id_type=MESH,
        )

    def c_first(t):
        spread(t, 0, fin[t], r1[t])

    def c_second(t):
        spread_all(t, 0, fin[t], r1[t]).wait_recv()
        for q in range(held):
            r2[t][0, q] = r1[t][offq[q], q]
            for e in range(1, nrow):
                send2[t][e, q] = r1[t][lax.rem(offq[q] - e + nrow, nrow), q]
        spread(t, 1, send2[t], r2[t])

    def c_end(t):
        spread_all(t, 1, send2[t], r2[t]).wait_recv()
        for o in range(held):
            q = qof[o]
            shift = sum(jnp.where(q == u, offq[u], 0) for u in range(held))
            for m in range(nrow):
                out[o, m, :, starts[t] : starts[t] + CHUNKS[t]] = r2[t][lax.rem(shift - m + nrow, nrow), q]

    for t in range(nt):
        a_own(t)
    turn(0, ncol // 2)
    a_part(0)
    a_pass(0, 0)
    turn(ncol // 2, ncol)
    a_pass(0, 1)
    loads["l"].wait()
    a_part(1)
    a_pass(1, 0)
    a_last(0, 0)
    a_last(0, 1)
    a_end(0)
    m1(0)
    a_pass(1, 1)
    b_first(0, 0)
    a_last(1, 0)
    b_first(0, 1)
    b_pass(0, 0)
    a_last(1, 1)
    b_first(0, 2)
    b_pass(0, 1)
    b_sum(0, 0)
    a_end(1)
    b_first(0, 3)
    b_pass(0, 2)
    b_sum(0, 1)
    m1(1)
    b_pass(0, 3)
    b_sum(0, 2)
    b_end(0, 0)
    b_first(1, 0)
    b_sum(0, 3)
    b_end(0, 1)
    b_first(1, 1)
    b_pass(1, 0)
    b_end(0, 2)
    b_first(1, 2)
    b_pass(1, 1)
    b_sum(1, 0)
    b_end(0, 3)
    c_first(0)
    b_first(1, 3)
    b_pass(1, 2)
    b_sum(1, 1)
    b_end(1, 0)
    c_second(0)
    b_pass(1, 3)
    b_sum(1, 2)
    b_end(1, 1)
    c_end(0)
    b_sum(1, 3)
    b_end(1, 2)
    b_end(1, 3)
    c_first(1)
    c_second(1)
    c_end(1)

    for copy in sent.values():
        copy.wait_send()
    for t in range(nt):
        spread_all(t, 0, fin[t], r1[t]).wait_send()
        spread_all(t, 1, send2[t], r2[t]).wait_send()


def on_device(vectors, right_factors, left_factors, tile_ranks, owner_map):
    held, ncol, blk, rank = right_factors.shape
    share, nvec = vectors.shape[1:]
    nrow, ndst = lax.axis_size("row"), lax.axis_size("col")
    sub = blk // ndst
    piece = sub // nrow
    nsend = len(CHUNKS) * (19 + 7 * held)
    scratch = [
        pltpu.VMEM((held, ncol, blk, rank), BF16),
        pltpu.VMEM((ncol, held * rank, blk), BF16),
        pltpu.VMEM((held, ncol, blk, rank), BF16),
        pltpu.SemaphoreType.DMA((nsend,)),
        pltpu.SemaphoreType.DMA((nsend,)),
        pltpu.SemaphoreType.DMA((len(CHUNKS) + ncol + 1,)),
        pltpu.SemaphoreType.DMA((len(CHUNKS), 2, 2)),
    ]
    for w in CHUNKS:
        scratch += [
            pltpu.VMEM((ncol, blk, w), BF16),
            pltpu.VMEM((held, ncol * rank, w), BF16),
            pltpu.VMEM((held, NYH, NZ, sub, w), BF16),
            pltpu.VMEM((held, 2, sub, w), BF16),
            pltpu.VMEM((held, 2, sub, w), BF16),
            pltpu.VMEM((held, 2, sub, w), BF16),
            pltpu.VMEM((held, sub, w), BF16),
            pltpu.VMEM((held, sub, w), F32),
            pltpu.VMEM((nrow, held, piece, w), BF16),
            pltpu.VMEM((nrow, held, piece, w), BF16),
            pltpu.VMEM((nrow, held, piece, w), BF16),
            pltpu.VMEM((nrow, held, piece, w), BF16),
            pltpu.SMEM((1,), I32),
        ]
    hbm = pl.BlockSpec(memory_space=pl.ANY)
    smem = pl.BlockSpec(memory_space=pltpu.SMEM)
    applied = pl.pallas_call(
        functools.partial(kernel, (held, ncol, blk, rank, share)),
        out_shape=jax.ShapeDtypeStruct((held, nrow, piece, nvec), BF16),
        in_specs=[hbm, hbm, hbm, smem, smem],
        out_specs=pl.BlockSpec(memory_space=pltpu.VMEM),
        scratch_shapes=scratch,
        compiler_params=pltpu.CompilerParams(
            collective_id=0, has_side_effects=True, vmem_limit_bytes=62 * 2**20
        ),
    )(vectors, right_factors, left_factors, tile_ranks, owner_map)
    return applied.reshape(held, sub, nvec)


def solution(mesh):
    placed = (
        P("col", "row", None),
        P("row", "col", None, None),
        P("row", "col", None, None),
        P("row", "col"),
        P(),
    )
    return jax.shard_map(
        on_device, mesh=mesh, in_specs=placed, out_specs=P("row", "col", None), check_vma=False
    )
```

time: 189 us -> 102 us (0.54)
  waiting for transfers between devices: 132 us -> 0 us
  Pallas kernels: 0 us -> 99.5 us
  matrix products: 16.4 us -> 0 us
  between operations: 13.4 us -> 0.01 us
  starting transfers between devices: 11.9 us -> 0 us
  other arithmetic: 6.68 us -> 0 us
  local copies, waits for them, and re-layouts: 6.76 us -> 1.87 us
    pallas_call x0 -> x1, Pallas kernels: none -> 99.5 us  [on_device(): pl.pallas_call(functools.partial(kernel, (held, ncol, blk, rank, share)),...]
    all_to_all x2 -> x0, waiting for transfers between devices: 75.1 us -> none  [the longest x1 48.5 us: sent_and_summed(): lax.all_to_all(pieces, axis, split_axis=0, concat_axis=0, tiled=True)]
    all_gather x1 -> x0, waiting for transfers between devices: 56.6 us -> none  [on_device(): lax.all_gather(vectors, 'row', axis=1, tiled=True)]
    dot_general x1 -> x0, matrix products: 16.4 us -> none  [on_device(): jnp.einsum('ikbr,ikrv->ibv', left_factors, coeffs, preferred_element_type...]
    all_to_all x2 -> x0, starting transfers between devices: 11.9 us -> none  [the longest x1 6.62 us: sent_and_summed(): lax.all_to_all(pieces, axis, split_axis=0, concat_axis=0, tiled=True)]
    reshape x1 -> x0, local copies, waits for them, and re-layouts: 5.27 us -> none  [split_up(): return jnp.moveaxis(x.reshape(*before, peers, -1, *after), dim, 0)]
    reduce_sum x3 -> x0, other arithmetic: 3.13 us -> none  [the longest x1 2.86 us: sent_and_summed(): return arrived.astype(jnp.float32).sum(axis=0)]
    select_n x5 -> x0, other arithmetic: 2.67 us -> none  [the longest x1 1.66 us: build_buffer(): return jnp.where(present[:, None, None], picked, jnp.zeros_like(picked))]
  transfers between devices with their start and end apart: 3 -> 0, of which waited for: 3 -> 0; matrix products, arithmetic and copies ran while one was open for 1% -> 0% of each run, Pallas kernels for 0% -> 0%
where the time goes in v1:
time: 102 us; the launch traced here: 101 us
  Pallas kernels  99.5 us (98%)
  local copies, waits for them, and re-layouts  1.87 us (2%)
    pallas_call x1, Pallas kernels, on_device(): pl.pallas_call(functools.partial(kernel, (held, ncol, blk, rank, share)),...  99.5 us

profile of v1, /device:TPU:1, one launch (start us, length us, event | category | flops | bytes accessed | tf_op | source)
XLA Modules:
  0.0 101.4 jit_solution(7256565301611170020)
XLA Ops:
  0.0 99.5 %shard_map.55 = bf16[4,16,8,512]{3,2,1,0:T(8,128)(2,1)} custom-call(bf16[8,64,512]{2,1,0:T(8,128)(2,1)} %refs_0_.1, bf16[4,8,1024,128]{3,2,1,0:T(8,128)(2,1)} %refs_1_.1, bf16[4,8,1024,128]{3,2,1,0:T(8,128)(2,1)} %refs_2_.1, s32[4,8]{1,0:T(4,128)} %refs_3_.1, s32[64]{0:T(128)} %refs_4_.1), custom_call_target="tpu_custom_call" | custom-call | tf_op jit(solution)/shard_map/pallas_call | solution.py:354
  99.5 1.9 %copy.7 = bf16[4,128,512]{2,1,0:T(8,128)(2,1)} copy(bf16[4,128,512]{2,1,0:T(8,128)(2,1)} %bitcast.1) | data formatting | bytes 1048576
